TPU v7x, 32 devices: a whole 2x2x4 slice. The times are simulated.
32 devices in a mesh: tile: 16 (over z, y, core), cam: 2 (over x).
Axes of the slice: x: 2, y: 2, z: 4, core: 2. Of those that a mesh axis runs over, the one named last changes fastest.
Arguments:
- features: bfloat16 [6144, 256], P(('tile', 'cam')), may hold values from -6 to 6
- value_weight: bfloat16 [256, 256], replicated, may hold values from -0.375 to 0.375
- output_weight: bfloat16 [256, 256], replicated, may hold values from -0.375 to 0.375
- hit_list: int32 [16, 2], P('tile'), may hold values from 0 to 5, as said below
- sample_index: int32 [8192, 2, 64], P('tile'), may hold values from 0 to 1023, as said below
- attention: bfloat16 [8192, 64], P('tile'), may hold values from 0.0099487305 to 1
- validity: int32 [8192, 2], P('tile'), may hold values from 0 to 1, as said below
Outputs:
- projected: bfloat16 [8192, 256], P(('tile', 'cam'))
Inputs may be any that keep to these rules, and one draw needn't show every extreme that they name: `hit_list`: camera numbers 0 to 5; where a tile sees one camera its two entries are equal. `validity`: where a tile's two hit_list entries are equal, the second column is 0 for every query of that tile. `sample_index`: for one query, slot and head, the 8 entries h * 8 to h * 8 + 7 all differ.
All inputs are finite; a program needn't handle non-finite values.
Results may differ from a plain program's by a relative error of at most 0.0058.
Values may be sent and summed in bfloat16 or wider, within the bound.
A program may use at most 64 MiB of HBM per device.

v0:
```python
import functools

import jax
import jax.numpy as jnp
from jax import lax
from jax.experimental import pallas as pl
from jax.experimental.pallas import tpu as pltpu
from jax.sharding import PartitionSpec as P

H = 8
K = 8
HITS = 2
CAM_ROWS = 1024
LANES = 128
MESH = pl.DeviceIdType.MESH


def gather_kernel(depth, v_ref, G, recv, sx, sz, sy, sc):
    me = lax.axis_index("tile")
    x = lax.axis_index("cam")
    core = lax.rem(me, 2)
    y = lax.rem(me // 2, 2)
    z = me // 4
    rows, width = G.shape[0] // (depth * 8), G.shape[1]

    def half_of(index):
        return v_ref.at[:, pl.ds(pl.multiple_of(index * width, width), width)]

    def place(zz, yy, cc):
        return (zz * 2 + yy) * 2 + cc

    def block_of(zz, yy, cc, b):
        return place(zz, yy, cc) * 2 + b

    def span(blk):
        return pl.ds(pl.multiple_of(blk * rows, 16), rows)

    has_up = z < depth - 1
    has_down = z > 0
    x_peer = (me, 1 - x)
    y_peer = (place(z, 1 - y, core), x)
    c_peer = (place(z, y, 1 - core), x)
    has_up2 = z < depth - 2
    has_down2 = z > 1
    up_peer = (place(jnp.minimum(z + 1, depth - 1), y, core), x)
    down_peer = (place(jnp.maximum(z - 1, 0), y, core), x)
    up2_peer = (place(jnp.minimum(z + 2, depth - 1), y, core), x)
    down2_peer = (place(jnp.maximum(z - 2, 0), y, core), x)
    line = (
        (has_up2, up2_peer),
        (has_down2, down2_peer),
        (has_up, up_peer),
        (has_down, down_peer),
    )

    barrier = pltpu.get_barrier_semaphore()
    for peer in (x_peer, y_peer, c_peer):
        pl.semaphore_signal(barrier, inc=1, device_id=peer, device_id_type=MESH)

    peers = 3
    for exists, peer in line:
        peers = peers + exists.astype(jnp.int32)

        @pl.when(exists)
        def _(peer=peer):
            pl.semaphore_signal(barrier, inc=1, device_id=peer, device_id_type=MESH)

    pl.semaphore_wait(barrier, peers)

    def copy(src, blk, send, peer):
        return pltpu.make_async_remote_copy(
            src_ref=src,
            dst_ref=G.at[span(blk)],
            send_sem=send,
            recv_sem=recv.at[blk],
            device_id=peer,
            device_id_type=MESH,
        )

    def arrived(blk):
        copy(G.at[span(blk)], blk, sx.at[0], x_peer).wait_recv()

    own = block_of(z, y, core, x)
    copy(half_of(1 - x), own, sx.at[0], x_peer).start()

    def send_line(which, src, blk, slot):
        exists, peer = line[which]

        @pl.when(exists)
        def _():
            copy(src, blk, sz.at[slot], peer).start()

    def line_step(distance):
        for sign in (1, -1) if distance else (0,):
            zz = z - sign * distance
            live = (zz >= 0) & (zz < depth)
            for b in (0, 1):
                half = x if b == 0 else 1 - x

                def go(zz=zz, half=half, b=b, sign=sign):
                    blk = block_of(zz, y, core, half)
                    if distance == 0 and b == 0:
                        src = half_of(x)
                    else:
                        arrived(blk)
                        src = G.at[span(blk)]
                    slot = zz * 2 + half
                    if distance == 0:
                        for which in range(4):
                            send_line(which, src, blk, which * 2 + b)
                    elif distance == 2:
                        which = 2 if sign > 0 else 3
                        send_line(which, src, blk, 4 + which * 2 + b)
                    copy(src, blk, sy.at[slot], y_peer).start()
                    copy(src, blk, sc.at[slot], c_peer).start()

                if distance:
                    pl.when(live)(go)
                else:
                    go()

    def across_step(distance):
        for sign in (1, -1) if distance else (0,):
            zz = z - sign * distance
            live = (zz >= 0) & (zz < depth)
            for b in (0, 1):
                half = x if b == 0 else 1 - x

                def go(zz=zz, half=half):
                    blk = block_of(zz, 1 - y, core, half)
                    arrived(blk)
                    slot = depth * 2 + zz * 2 + half
                    copy(G.at[span(blk)], blk, sc.at[slot], c_peer).start()

                if distance:
                    pl.when(live)(go)
                else:
                    go()

    for distance in range(depth):
        line_step(distance)
        if distance:
            across_step(distance - 1)
    G[span(own), :] = v_ref[:, pl.ds(pl.multiple_of(x * width, width), width)]
    across_step(depth - 1)

    for zz in range(depth):
        for yy in (0, 1):
            for b in (0, 1):
                arrived(block_of(zz, yy, 1 - core, b))

    def sent(sem):
        copy(half_of(0), own, sem, x_peer).wait_send()

    sent(sx.at[0])
    for slot in range(depth * 2):
        sent(sy.at[slot])
    for b in (0, 1):
        for which in range(4):
            pl.when(line[which][0])(lambda i=which * 2 + b: sent(sz.at[i]))
        pl.when(has_up & has_down2)(lambda b=b: sent(sz.at[8 + b]))
        pl.when(has_down & has_up2)(lambda b=b: sent(sz.at[10 + b]))
    for slot in range(depth * 4):
        sent(sc.at[slot])


def gather_values(values, tiles):
    depth = tiles // 4
    rows, width = values.shape[0], values.shape[1] // 2
    blocks = tiles * 2
    dma = pltpu.SemaphoreType.DMA
    return pl.pallas_call(
        functools.partial(gather_kernel, depth),
        out_shape=jax.ShapeDtypeStruct((blocks * rows, width), jnp.bfloat16),
        in_specs=[pl.BlockSpec(memory_space=pltpu.VMEM)],
        out_specs=pl.BlockSpec(memory_space=pltpu.VMEM),
        scratch_shapes=[
            dma((blocks,)),
            dma((1,)),
            dma((12,)),
            dma((depth * 2,)),
            dma((depth * 4,)),
        ],
        compiler_params=pltpu.CompilerParams(collective_id=0, has_side_effects=True),
    )(values)


def lane_pick(source, index):
    return jnp.take_along_axis(source, index, axis=1, mode="promise_in_bounds")


def sample_kernel(
    heads, pair, hit_ref, head_ref, vals_ref, idx_ref, attn_ref, valid_ref, out_ref, table, attns, summed
):
    width = vals_ref.shape[1]
    head_width = width // heads
    queries = idx_ref.shape[1]
    groups = queries // LANES
    parts = CAM_ROWS // LANES
    for s in range(HITS):
        for j in range(parts):
            first = pl.multiple_of(hit_ref[0, s] * CAM_ROWS + j * LANES, LANES)
            block = vals_ref[pl.ds(first, LANES), :].astype(jnp.float32)
            table[s * parts + j] = block.T
    attns[...] = attn_ref[...].astype(jnp.float32)

    def one(step, _):
        g = step * pair // heads
        lanes = pl.ds(pl.multiple_of(g * LANES, LANES), LANES)
        valid = valid_ref[:, lanes]
        count = jnp.maximum(jnp.sum(valid, axis=0, keepdims=True), 1)
        factor = valid.astype(jnp.float32) * (1.0 / count.astype(jnp.float32))
        for e in range(pair):
            h = lax.rem(step * pair, heads) + e
            attn = attns[pl.ds(pl.multiple_of((head_ref[0] + h) * K, K), K), lanes]
            acc = [jnp.zeros((8, LANES), jnp.float32)] * (head_width // 8)
            for s in range(HITS):
                index = idx_ref[pl.ds(pl.multiple_of(s * heads * K + h * K, K), K), lanes]
                low = index & (LANES - 1)
                high = index // LANES
                weight = attn * factor[s : s + 1]
                for k in range(K):
                    lo = jnp.broadcast_to(low[k : k + 1], (8, LANES))
                    hi = jnp.broadcast_to(high[k : k + 1], (8, LANES))
                    wt = jnp.broadcast_to(weight[k : k + 1], (8, LANES))
                    masks = [hi == j for j in range(parts)]
                    for d in range(head_width // 8):
                        cols = pl.ds(pl.multiple_of(h * head_width + d * 8, 8), 8)
                        picked = lane_pick(table[s * parts, cols, :], lo)
                        for j in range(1, parts):
                            got = lane_pick(table[s * parts + j, cols, :], lo)
                            picked = jnp.where(masks[j], got, picked)
                        acc[d] = acc[d] + wt * picked
            for d in range(head_width // 8):
                summed[pl.ds(pl.multiple_of(h * head_width + d * 8, 8), 8), :] = acc[d]

        @pl.when(lax.rem(step * pair, heads) == heads - pair)
        def _():
            rows = pl.ds(pl.multiple_of(g * LANES, LANES), LANES)
            out_ref[rows, :] = summed[...].T.astype(out_ref.dtype)

        return 0

    lax.fori_loop(0, groups * heads // pair, one, 0)


def sample(hit_list, vals, index, attention, validity, heads, first_head):
    queries = index.shape[0]
    width = vals.shape[1]
    padded = -(-queries // LANES) * LANES
    index = index.reshape(queries, HITS * heads * K).T
    extra = padded - queries
    index = jnp.pad(index, ((0, 0), (0, extra)))
    validity = jnp.pad(validity.T, ((0, 0), (0, extra)))
    attention = jnp.pad(attention.T, ((0, 0), (0, extra)))
    pair = 4 if heads % 4 == 0 else 1
    first_head = jnp.reshape(first_head, (1,)).astype(jnp.int32)
    out = pl.pallas_call(
        functools.partial(sample_kernel, heads, pair),
        out_shape=jax.ShapeDtypeStruct((padded, width), jnp.bfloat16),
        in_specs=[pl.BlockSpec(memory_space=pltpu.SMEM)] * 2
        + [pl.BlockSpec(memory_space=pltpu.VMEM)] * 4,
        out_specs=pl.BlockSpec(memory_space=pltpu.VMEM),
        scratch_shapes=[
            pltpu.VMEM((HITS * CAM_ROWS // LANES, width, LANES), jnp.float32),
            pltpu.VMEM(attention.shape, jnp.float32),
            pltpu.VMEM((width, LANES), jnp.float32),
        ],
    )(hit_list, first_head, vals, index, attention, validity)
    return out[:queries]


def exchange_kernel(a_ref, out_ref, local, send, recv):
    me = lax.axis_index("tile")
    x = lax.axis_index("cam")
    rows = out_ref.shape[0]
    width = a_ref.shape[1]
    peer = (me, 1 - x)
    barrier = pltpu.get_barrier_semaphore()
    pl.semaphore_signal(barrier, inc=1, device_id=peer, device_id_type=MESH)
    pl.semaphore_wait(barrier, 1)

    def share(index):
        return a_ref.at[pl.ds(pl.multiple_of(index * rows, rows), rows)]

    mine = out_ref.at[:, pl.ds(pl.multiple_of(x * width, width), width)]
    copy = pltpu.make_async_remote_copy(
        src_ref=share(1 - x),
        dst_ref=mine,
        send_sem=send,
        recv_sem=recv,
        device_id=peer,
        device_id_type=MESH,
    )
    copy.start()
    keep = pltpu.make_async_copy(share(x), mine, local)
    keep.start()
    keep.wait()
    copy.wait()


def exchange(attended):
    queries, width = attended.shape
    dma = pltpu.SemaphoreType.DMA
    return pl.pallas_call(
        exchange_kernel,
        out_shape=jax.ShapeDtypeStruct((queries // 2, width * 2), jnp.bfloat16),
        in_specs=[pl.BlockSpec(memory_space=pltpu.VMEM)],
        out_specs=pl.BlockSpec(memory_space=pltpu.VMEM),
        scratch_shapes=[dma, dma, dma],
        compiler_params=pltpu.CompilerParams(collective_id=1, has_side_effects=True),
    )(attended)


def body(features, value_weight, output_weight, hit_list, sample_index, attention, validity):
    values = jnp.dot(features, value_weight, preferred_element_type=jnp.float32).astype(
        jnp.bfloat16
    )
    tiles = lax.axis_size("tile")
    cams = lax.axis_size("cam")
    place = lax.axis_index("cam")
    queries = sample_index.shape[0]
    width = values.shape[1]
    if cams == 2 and tiles in (4, 8, 12, 16) and width == 2 * LANES and features.shape[0] % 16 == 0:
        heads = H // 2
        vals = gather_values(values, tiles)
        index = lax.dynamic_slice_in_dim(sample_index, place * heads * K, heads * K, 2)
        attended = sample(
            hit_list, vals, index, attention, validity, heads, place * heads
        )
        attended = exchange(attended)
    else:
        share = queries // cams
        everything = lax.all_gather(values, ("tile", "cam"), axis=0, tiled=True)
        index, weights, valid = (
            lax.dynamic_slice_in_dim(a, place * share, share, 0)
            for a in (sample_index, attention, validity)
        )
        attended = sample(hit_list, everything, index, weights, valid, H, jnp.int32(0))
    return jnp.dot(attended, output_weight, preferred_element_type=jnp.float32).astype(jnp.bfloat16)


def solution(mesh):
    in_specs = (
        P(("tile", "cam"), None),
        P(),
        P(),
        P("tile", None),
        P("tile", None, None),
        P("tile", None),
        P("tile", None),
    )
    out_specs = P(("tile", "cam"), None)
    return jax.shard_map(body, mesh=mesh, in_specs=in_specs, out_specs=out_specs, check_vma=False)
```

profile of v0, /device:TPU:0, one launch (start us, length us, event | category | flops | bytes accessed | tf_op | source)
XLA Modules:
  0.0 45.7 jit_solution(6853161792910880231)
XLA Ops:
  0.0 0.0 copy-start
  0.0 1.8 %convolution_convert_fusion.1.v_ref = bf16[192,256]{1,0:T(8,128)(2,1)} fusion(bf16[192,256]{1,0:T(8,128)(2,1)} %param.7, bf16[256,256]{1,0:T(8,128)(2,1)} %param.8), kind=kOutput, calls=%fused_computation.1 | convolution fusion | flops 25214976 | bytes 327680 | tf_op jit(solution)/shard_map/dot_general | solution.py:316
  1.8 0.0 copy-done
  1.8 0.7 %constant_dynamic-slice_fusion = s32[512,2,32]{0,2,1:T(8,128)} fusion(s32[512,2,64]{0,2,1:T(8,128)S(1)} %copy-done, s32[]{:T(128)S(6)} %select_n.3), kind=kLoop, calls=%fused_computation.2 | loop fusion | bytes 262148 | tf_op jit(solution)/shard_map/dynamic_slice | solution.py:327
  2.5 0.0 copy-start.1
  2.5 22.7 %shard_map.73.vals_ref = bf16[6144,128]{1,0:T(8,128)(2,1)} custom-call(bf16[192,256]{1,0:T(8,128)(2,1)} %convolution_convert_fusion.1.v_ref), custom_call_target="tpu_custom_call" | custom-call | tf_op jit(solution)/shard_map/pallas_call | solution.py:172
  25.2 12.8 %shard_map.74.a_ref = bf16[512,128]{1,0:T(8,128)(2,1)} custom-call(s32[1,2]{1,0:T(1,128)} %hit_ref.1, s32[1]{0:T(128)} %bitcast.head_ref, bf16[6144,128]{1,0:T(8,128)(2,1)} %shard_map.73.vals_ref, s32[64,512]{1,0:T(8,128)} %bitcast.10, bf16[64,512]{1,0:T(8,128)(2,1)} %bitcast.11, s32[2,512]{1,0:T(2,128)} %bitcast.12), custom_call_target="tpu_custom_call" | custom-call | tf_op jit(solution)/shard_map/pallas_call | solution.py:258
  38.0 6.0 %shard_map.75 = bf16[256,256]{1,0:T(8,128)(2,1)} custom-call(bf16[512,128]{1,0:T(8,128)(2,1)} %shard_map.74.a_ref), custom_call_target="tpu_custom_call" | custom-call | tf_op jit(solution)/shard_map/pallas_call | solution.py:305
  43.9 0.0 copy-done.1
  43.9 1.7 %convolution_convert_fusion = bf16[256,256]{1,0:T(8,128)(2,1)} fusion(bf16[256,256]{1,0:T(8,128)(2,1)} %shard_map.75, bf16[256,256]{1,0:T(8,128)(2,1)S(1)} %copy-done.1), kind=kOutput, calls=%fused_computation | convolution fusion | flops 33619968 | bytes 393216 | tf_op jit(solution)/shard_map/dot_general | solution.py:340
Async XLA Ops:
  0.0 1.8 %copy-start = (s32[512,2,64]{0,2,1:T(8,128)S(1)}, s32[512,2,64]{0,2,1:T(8,128)}, u32[]{:S(2)}) copy-start(s32[512,2,64]{0,2,1:T(8,128)} %param.11) | copy-start | bytes 786436
  2.5 41.5 %copy-start.1 = (bf16[256,256]{1,0:T(8,128)(2,1)S(1)}, bf16[256,256]{1,0:T(8,128)(2,1)}, u32[]{:S(2)}) copy-start(bf16[256,256]{1,0:T(8,128)(2,1)} %param.9) | copy-start | bytes 393220
where the time goes:
time: 45.9 us; the launch traced here: 45.7 us
  Pallas kernels  41.4 us (90%)
  matrix products  3.55 us (8%)
  local copies, waits for them, and re-layouts  0.67 us (1%)
    pallas_call x1, Pallas kernels, gather_values(): pl.pallas_call(functools.partial(gather_kernel, depth), out_shape=jax.Sha...  22.7 us
    pallas_call x1, Pallas kernels, sample(): pl.pallas_call(functools.partial(sample_kernel, heads, pair), out_shape=j...  12.8 us
    pallas_call x1, Pallas kernels, exchange(): pl.pallas_call(exchange_kernel, out_shape=jax.ShapeDtypeStruct((queries /...  5.95 us
    dot_general x1, matrix products, body(): jnp.dot(features, value_weight, preferred_element_type=jnp.float32)  1.81 us
    dot_general x1, matrix products, body(): jnp.dot(attended, output_weight, preferred_element_type=jnp.float32)  1.75 us

commit v1 on v0

v1 whole, which is shorter than its diff:
```python
import functools

import jax
import jax.numpy as jnp
from jax import lax
from jax.experimental import pallas as pl
from jax.experimental.pallas import tpu as pltpu
from jax.sharding import PartitionSpec as P

H = 8
K = 8
HITS = 2
CAMS = 6
CAM_ROWS = 1024
LANES = 128
PACK = 16
MESH = pl.DeviceIdType.MESH


class Plan:
    def __init__(self, tiles, rows, queries, width):
        self.tiles, self.rows, self.queries, self.width = tiles, rows, queries, width
        self.depth = tiles // 4
        self.chunks = 4
        self.piece = rows // self.chunks
        self.total = tiles * rows
        firsts = [[self.first(c * CAM_ROWS, x) for c in range(CAMS + 1)] for x in (0, 1)]
        extent = max(f[c + 1] - f[c] for f in firsts for c in range(CAMS))
        self.span = -(-extent // PACK) * PACK
        self.starts = [[min(f[c], self.total - self.span) for c in range(CAMS)] for f in firsts]
        self.shift = 20
        self.factor = -(-(1 << self.shift) // rows)

    def first(self, row, x):
        pair = 2 * self.rows
        return row // pair * self.rows + min(max(row % pair - x * self.rows, 0), self.rows)

    def fits(self):
        everything = CAMS * CAM_ROWS
        return (
            2 * self.total == everything
            and self.rows % (self.chunks * PACK) == 0
            and all(s % PACK == 0 for f in self.starts for s in f)
            and everything * self.factor < 1 << 31
            and all((r * self.factor) >> self.shift == r // self.rows for r in range(everything))
            and self.queries % (2 * LANES) == 0
            and self.width == 2 * LANES
        )


def fused_kernel(
    plan, hit_ref, feat_hbm, wv_hbm, wo_hbm, idx_hbm, attn_hbm, valid_hbm, out_ref,
    G, wv, wo, wvt, idx, attn, valid, weights, table, cells, vt, kept, outgoing, incoming,
    local, recv, sup, sdown, sy, sc, sx, rx,
):
    me = lax.axis_index("tile")
    x = lax.axis_index("cam")
    core = lax.rem(me, 2)
    y = lax.rem(me // 2, 2)
    z = me // 4
    depth, chunks, piece, rows = plan.depth, plan.chunks, plan.piece, plan.rows
    span, queries, width = plan.span, plan.queries, plan.width
    head_width = width // H
    share = queries // 2

    def place(zz, yy, cc):
        return (zz * 2 + yy) * 2 + cc

    def part(blk, j):
        return pl.ds(pl.multiple_of(blk * rows + j * piece, PACK), piece)

    own = place(z, y, core)
    load_feat = pltpu.make_async_copy(
        feat_hbm, G.at[pl.ds(pl.multiple_of(own * rows, PACK), rows)], local.at[0]
    )
    load_feat.start()
    loads = [
        pltpu.make_async_copy(src, dst, local.at[i + 1])
        for i, (src, dst) in enumerate(
            ((idx_hbm, idx), (attn_hbm, attn), (valid_hbm, valid), (wv_hbm, wv), (wo_hbm, wo))
        )
    ]
    for load in loads:
        load.start()

    has_up = z < depth - 1
    has_down = z > 0
    x_peer = (me, 1 - x)
    y_peer = (place(z, 1 - y, core), x)
    c_peer = (place(z, y, 1 - core), x)
    up_peer = (place(jnp.minimum(z + 1, depth - 1), y, core), x)
    down_peer = (place(jnp.maximum(z - 1, 0), y, core), x)

    barrier = pltpu.get_barrier_semaphore()
    for peer in (x_peer, y_peer, c_peer):
        pl.semaphore_signal(barrier, inc=1, device_id=peer, device_id_type=MESH)
    peers = 3
    for exists, peer in ((has_up, up_peer), (has_down, down_peer)):
        peers = peers + exists.astype(jnp.int32)

        @pl.when(exists)
        def _(peer=peer):
            pl.semaphore_signal(barrier, inc=1, device_id=peer, device_id_type=MESH)

    pl.semaphore_wait(barrier, peers)

    def copy(blk, j, send, peer):
        ref = G.at[part(blk, j)]
        return pltpu.make_async_remote_copy(
            src_ref=ref,
            dst_ref=ref,
            send_sem=send,
            recv_sem=recv.at[blk * chunks + j],
            device_id=peer,
            device_id_type=MESH,
        )

    def arrived(blk, j):
        copy(blk, j, sy.at[0], x_peer).wait_recv()

    def send_up(zz, j):
        @pl.when(has_up)
        def _():
            copy(place(zz, y, core), j, sup.at[zz * chunks + j], up_peer).start()

    def send_down(zz, j):
        @pl.when(has_down)
        def _():
            copy(place(zz, y, core), j, sdown.at[zz * chunks + j], down_peer).start()

    def send_y(zz, j):
        copy(place(zz, y, core), j, sy.at[zz * chunks + j], y_peer).start()

    def send_c(zz, across, j):
        yy = 1 - y if across else y
        slot = (zz * 2 + across) * chunks + j
        copy(place(zz, yy, core), j, sc.at[slot], c_peer).start()

    load_feat.wait()
    for j in range(chunks):
        send_up(z, j)
        send_down(z, j)
        send_y(z, j)
    for j in range(chunks):
        send_c(z, 0, j)

    for load in loads:
        load.wait()
    wvt[...] = wv[...].T
    count = jnp.maximum(jnp.sum(valid[...], axis=0, keepdims=True), 1)
    factor = valid[...].astype(jnp.float32) * (1.0 / count.astype(jnp.float32))
    scores = attn[...].astype(jnp.float32)
    starts = [jnp.where(x == 0, plan.starts[0][c], plan.starts[1][c]) for c in range(CAMS)]
    for s in range(HITS):
        hit = jnp.full((1, queries), hit_ref[0, s], jnp.int32)
        start = jnp.full((1, queries), starts[0], jnp.int32)
        for c in range(1, CAMS):
            start = jnp.where(hit == c, starts[c], start)
        points = slice(s * H * K, (s + 1) * H * K)
        row = idx[points, :] + hit * CAM_ROWS
        blk = (row * plan.factor) >> plan.shift
        near = (blk >> 1) * rows + row - blk * rows - start
        idx[points, :] = jnp.where((blk & 1) == x, near, -1)
        weights[points, :] = scores * factor[s : s + 1]

    blocks = queries // LANES
    units = H * HITS * blocks

    def unit(u, _):
        h = u // (HITS * blocks)
        s = lax.rem(u // blocks, HITS)
        lanes = pl.ds(pl.multiple_of(lax.rem(u, blocks) * LANES, LANES), LANES)
        points = pl.ds(pl.multiple_of(s * H * K + h * K, K), K)
        at = idx[points, lanes]
        wt = weights[points, lanes]
        ats = [jnp.broadcast_to(at[k : k + 1], (PACK, LANES)).astype(jnp.int16) for k in range(K)]
        wts = [jnp.broadcast_to(wt[k : k + 1], (PACK, LANES)).astype(jnp.bfloat16) for k in range(K)]
        lane_row = lax.broadcasted_iota(jnp.int32, (PACK, LANES), 0).astype(jnp.int16)
        for j in range(span // PACK):
            here = lane_row + jnp.int16(j * PACK)
            cell = jnp.zeros((PACK, LANES), jnp.bfloat16)
            for k in range(K):
                cell = jnp.where(ats[k] == here, wts[k], cell)
            first = pl.multiple_of((h * HITS + s) * span + j * PACK, PACK)
            table[pl.ds(first, PACK), lanes] = cell
        return 0

    done = [0]

    def build(count):
        count = min(count, units - done[0])
        if count > 0:
            lax.fori_loop(done[0], done[0] + count, unit, 0)
            done[0] += count

    FIRST, STEP = plan.pace
    build(FIRST)
    for wave in range(1, depth + 1):
        for j in range(chunks):
            for sign in (1, -1):
                if wave < depth:
                    zz = z - sign * wave
                    live = (zz >= 0) & (zz < depth)

                    @pl.when(live)
                    def _(zz=zz, sign=sign, j=j):
                        arrived(place(zz, y, core), j)
                        (send_up if sign > 0 else send_down)(zz, j)
                        send_y(zz, j)
                        send_c(zz, 0, j)

            for sign in (1, -1) if wave > 1 else (0,):
                zz = z - sign * (wave - 1)
                live = (zz >= 0) & (zz < depth)

                def go(zz=zz, j=j):
                    arrived(place(zz, 1 - y, core), j)
                    send_c(zz, 1, j)

                if wave > 1:
                    pl.when(live)(go)
                else:
                    go()
            build(STEP)
    build(units)

    for zz in range(depth):
        for yy in (0, 1):
            for j in range(chunks):
                arrived(place(zz, yy, 1 - core), j)

    picks = []
    for s in range(HITS):
        hit = jnp.full((PACK, width), hit_ref[0, s], jnp.int32)
        picks.append([(hit == c).astype(jnp.float32).astype(jnp.bfloat16) for c in range(CAMS)])
    for j in range(span // PACK):
        found = [jnp.zeros((PACK, width), jnp.bfloat16)] * HITS
        for c in range(CAMS):
            block = G[pl.ds(pl.multiple_of(starts[c] + j * PACK, PACK), PACK), :]
            found = [found[s] + block * picks[s][c] for s in range(HITS)]
        for s in range(HITS):
            cells[s * span + j * PACK : s * span + (j + 1) * PACK, :] = found[s]
    vt[...] = lax.dot_general(
        wvt[...], cells[...], (((1,), (1,)), ((), ())), preferred_element_type=jnp.float32
    ).astype(jnp.bfloat16)

    def sampled(h, half):
        lanes = pl.ds(pl.multiple_of(half * share, share), share)
        block = table[h * HITS * span : (h + 1) * HITS * span, lanes]
        return jnp.dot(
            vt[h * head_width : (h + 1) * head_width, :], block, preferred_element_type=jnp.float32
        )

    group = 2

    def cross(i):
        rows_i = pl.ds(i * group * head_width, group * head_width)
        return pltpu.make_async_remote_copy(
            src_ref=outgoing.at[rows_i],
            dst_ref=incoming.at[rows_i],
            send_sem=sx.at[i],
            recv_sem=rx.at[i],
            device_id=x_peer,
            device_id_type=MESH,
        )

    for h in range(H):
        outgoing[h * head_width : (h + 1) * head_width, :] = sampled(h, 1 - x).astype(jnp.bfloat16)
        if h % group == group - 1:
            cross(h // group).start()
    for h in range(H):
        kept[h * head_width : (h + 1) * head_width, :] = sampled(h, x)

    for i in range(H // group):
        cross(i).wait_recv()
    attended = (kept[...] + incoming[...].astype(jnp.float32)).astype(jnp.bfloat16)
    out_ref[...] = lax.dot_general(
        attended, wo[...], (((0,), (0,)), ((), ())), preferred_element_type=jnp.float32
    ).astype(out_ref.dtype)

    def sent(sem):
        copy(own, 0, sem, x_peer).wait_send()

    for zz in range(depth):
        for j in range(chunks):
            slot = zz * chunks + j
            pl.when(has_up & (zz <= z))(lambda slot=slot: sent(sup.at[slot]))
            pl.when(has_down & (zz >= z))(lambda slot=slot: sent(sdown.at[slot]))
            sent(sy.at[slot])
    for slot in range(depth * 2 * chunks):
        sent(sc.at[slot])
    for i in range(H // group):
        cross(i).wait_send()


def fused(plan, features, value_weight, output_weight, hit_list, index, attention, validity):
    queries, width = plan.queries, plan.width
    dma = pltpu.SemaphoreType.DMA
    points = HITS * H * K
    slots = plan.depth * plan.chunks
    bf16, f32 = jnp.bfloat16, jnp.float32
    index = index.reshape(queries, points).T
    return pl.pallas_call(
        functools.partial(fused_kernel, plan),
        out_shape=jax.ShapeDtypeStruct((queries // 2, width), bf16),
        in_specs=[pl.BlockSpec(memory_space=pltpu.SMEM)] + [pl.BlockSpec(memory_space=pl.ANY)] * 6,
        out_specs=pl.BlockSpec(memory_space=pltpu.VMEM),
        scratch_shapes=[
            pltpu.VMEM((plan.total, width), bf16),
            pltpu.VMEM((width, width), bf16),
            pltpu.VMEM((width, width), bf16),
            pltpu.VMEM((width, width), bf16),
            pltpu.VMEM((points, queries), jnp.int32),
            pltpu.VMEM((H * K, queries), bf16),
            pltpu.VMEM((HITS, queries), jnp.int32),
            pltpu.VMEM((points, queries), f32),
            pltpu.VMEM((H * HITS * plan.span, queries), bf16),
            pltpu.VMEM((HITS * plan.span, width), bf16),
            pltpu.VMEM((width, HITS * plan.span), bf16),
            pltpu.VMEM((width, queries // 2), f32),
            pltpu.VMEM((width, queries // 2), bf16),
            pltpu.VMEM((width, queries // 2), bf16),
            dma((6,)),
            dma((plan.tiles * plan.chunks,)),
            dma((slots,)),
            dma((slots,)),
            dma((slots,)),
            dma((slots * 2,)),
            dma((H // 2,)),
            dma((H // 2,)),
        ],
        compiler_params=pltpu.CompilerParams(
            collective_id=0, has_side_effects=True, vmem_limit_bytes=40 << 20
        ),
    )(hit_list, features, value_weight, output_weight, index, attention.T, validity.T)


def lane_pick(source, index):
    return jnp.take_along_axis(source, index, axis=1, mode="promise_in_bounds")


def sample_kernel(
    heads, pair, hit_ref, head_ref, vals_ref, idx_ref, attn_ref, valid_ref, out_ref, table, attns, summed
):
    width = vals_ref.shape[1]
    head_width = width // heads
    queries = idx_ref.shape[1]
    groups = queries // LANES
    parts = CAM_ROWS // LANES
    for s in range(HITS):
        for j in range(parts):
            first = pl.multiple_of(hit_ref[0, s] * CAM_ROWS + j * LANES, LANES)
            block = vals_ref[pl.ds(first, LANES), :].astype(jnp.float32)
            table[s * parts + j] = block.T
    attns[...] = attn_ref[...].astype(jnp.float32)

    def one(step, _):
        g = step * pair // heads
        lanes = pl.ds(pl.multiple_of(g * LANES, LANES), LANES)
        valid = valid_ref[:, lanes]
        count = jnp.maximum(jnp.sum(valid, axis=0, keepdims=True), 1)
        factor = valid.astype(jnp.float32) * (1.0 / count.astype(jnp.float32))
        for e in range(pair):
            h = lax.rem(step * pair, heads) + e
            attn = attns[pl.ds(pl.multiple_of((head_ref[0] + h) * K, K), K), lanes]
            acc = [jnp.zeros((8, LANES), jnp.float32)] * (head_width // 8)
            for s in range(HITS):
                index = idx_ref[pl.ds(pl.multiple_of(s * heads * K + h * K, K), K), lanes]
                low = index & (LANES - 1)
                high = index // LANES
                weight = attn * factor[s : s + 1]
                for k in range(K):
                    lo = jnp.broadcast_to(low[k : k + 1], (8, LANES))
                    hi = jnp.broadcast_to(high[k : k + 1], (8, LANES))
                    wt = jnp.broadcast_to(weight[k : k + 1], (8, LANES))
                    masks = [hi == j for j in range(parts)]
                    for d in range(head_width // 8):
                        cols = pl.ds(pl.multiple_of(h * head_width + d * 8, 8), 8)
                        picked = lane_pick(table[s * parts, cols, :], lo)
                        for j in range(1, parts):
                            got = lane_pick(table[s * parts + j, cols, :], lo)
                            picked = jnp.where(masks[j], got, picked)
                        acc[d] = acc[d] + wt * picked
            for d in range(head_width // 8):
                summed[pl.ds(pl.multiple_of(h * head_width + d * 8, 8), 8), :] = acc[d]

        @pl.when(lax.rem(step * pair, heads) == heads - pair)
        def _():
            rows = pl.ds(pl.multiple_of(g * LANES, LANES), LANES)
            out_ref[rows, :] = summed[...].T.astype(out_ref.dtype)

        return 0

    lax.fori_loop(0, groups * heads // pair, one, 0)


def sample(hit_list, vals, index, attention, validity, heads, first_head):
    queries = index.shape[0]
    width = vals.shape[1]
    padded = -(-queries // LANES) * LANES
    index = index.reshape(queries, HITS * heads * K).T
    extra = padded - queries
    index = jnp.pad(index, ((0, 0), (0, extra)))
    validity = jnp.pad(validity.T, ((0, 0), (0, extra)))
    attention = jnp.pad(attention.T, ((0, 0), (0, extra)))
    pair = 4 if heads % 4 == 0 else 1
    first_head = jnp.reshape(first_head, (1,)).astype(jnp.int32)
    out = pl.pallas_call(
        functools.partial(sample_kernel, heads, pair),
        out_shape=jax.ShapeDtypeStruct((padded, width), jnp.bfloat16),
        in_specs=[pl.BlockSpec(memory_space=pltpu.SMEM)] * 2
        + [pl.BlockSpec(memory_space=pltpu.VMEM)] * 4,
        out_specs=pl.BlockSpec(memory_space=pltpu.VMEM),
        scratch_shapes=[
            pltpu.VMEM((HITS * CAM_ROWS // LANES, width, LANES), jnp.float32),
            pltpu.VMEM(attention.shape, jnp.float32),
            pltpu.VMEM((width, LANES), jnp.float32),
        ],
    )(hit_list, first_head, vals, index, attention, validity)
    return out[:queries]


def body(features, value_weight, output_weight, hit_list, sample_index, attention, validity):
    tiles = lax.axis_size("tile")
    cams = lax.axis_size("cam")
    place = lax.axis_index("cam")
    queries = sample_index.shape[0]
    rows, width = features.shape
    if cams == 2 and tiles in (4, 8, 12, 16):
        plan = Plan(tiles, rows, queries, width)
        plan.pace = (20, 4)
        if plan.fits():
            return fused(
                plan, features, value_weight, output_weight, hit_list, sample_index, attention, validity
            )
    values = jnp.dot(features, value_weight, preferred_element_type=jnp.float32).astype(jnp.bfloat16)
    share = queries // cams
    everything = lax.all_gather(values, ("tile", "cam"), axis=0, tiled=True)
    index, weights, valid = (
        lax.dynamic_slice_in_dim(a, place * share, share, 0)
        for a in (sample_index, attention, validity)
    )
    attended = sample(hit_list, everything, index, weights, valid, H, jnp.int32(0))
    return jnp.dot(attended, output_weight, preferred_element_type=jnp.float32).astype(jnp.bfloat16)


def solution(mesh):
    in_specs = (
        P(("tile", "cam"), None),
        P(),
        P(),
        P("tile", None),
        P("tile", None, None),
        P("tile", None),
        P("tile", None),
    )
    out_specs = P(("tile", "cam"), None)
    return jax.shard_map(body, mesh=mesh, in_specs=in_specs, out_specs=out_specs, check_vma=False)
```

time: 45.9 us -> 33.2 us (0.72)
  Pallas kernels: 41.4 us -> 27.1 us
  local copies, waits for them, and re-layouts: 0.67 us -> 5.83 us
  matrix products: 3.55 us -> 0 us
    pallas_call x3 -> x1, Pallas kernels: 41.4 us -> 27.1 us  [fused(): pl.pallas_call(functools.partial(fused_kernel, plan), out_shape=jax.Shape...]
    unnamed x4 -> x15, local copies, waits for them, and re-layouts: 0.01 us -> 5.83 us
    dot_general x2 -> x0, matrix products: 3.55 us -> none  [the longest x1 1.81 us: body(): jnp.dot(features, value_weight, preferred_element_type=jnp.float32)]
    dynamic_slice x1 -> x0, local copies, waits for them, and re-layouts: 0.66 us -> none  [body(): lax.dynamic_slice_in_dim(sample_index, place * heads * K, heads * K, 2)]
where the time goes in v1:
time: 33.2 us; the launch traced here: 33 us
  Pallas kernels  27.1 us (82%)
  local copies, waits for them, and re-layouts  5.83 us (18%)
    pallas_call x1, Pallas kernels, fused(): pl.pallas_call(functools.partial(fused_kernel, plan), out_shape=jax.Shape...  27.1 us
    unnamed x15, local copies, waits for them, and re-layouts  5.83 us

profile of v1, /device:TPU:0, one launch (start us, length us, event | category | flops | bytes accessed | tf_op | source)
XLA Modules:
  0.0 33.0 jit_solution(7498209913954644112)
XLA Ops:
  0.0 0.0 copy-start.5
  0.0 0.0 copy-start.6
  0.0 0.7 %copy-done.5 = s32[512,2]{0,1:T(2,128)S(1)} copy-done((s32[512,2]{0,1:T(2,128)S(1)}, s32[512,2]{0,1:T(2,128)}, u32[]{:S(2)}) %copy-start.5) | copy-done | bytes 4120
  0.7 0.0 copy-done.6
  0.7 0.0 copy-start
  0.7 0.9 %copy-done = s32[512,2,64]{0,2,1:T(8,128)S(1)} copy-done((s32[512,2,64]{0,2,1:T(8,128)S(1)}, s32[512,2,64]{0,2,1:T(8,128)}, u32[]{:S(2)}) %copy-start) | copy-done | bytes 262168
  1.6 0.0 copy-start.1
  1.6 0.9 %copy-done.1 = bf16[256,256]{1,0:T(8,128)(2,1)S(1)} copy-done((bf16[256,256]{1,0:T(8,128)(2,1)S(1)}, bf16[256,256]{1,0:T(8,128)(2,1)}, u32[]{:S(2)}) %copy-start.1) | copy-done | bytes 131096
  2.5 0.0 copy-start.2
  2.5 0.9 %copy-done.2 = bf16[256,256]{1,0:T(8,128)(2,1)S(1)} copy-done((bf16[256,256]{1,0:T(8,128)(2,1)S(1)}, bf16[256,256]{1,0:T(8,128)(2,1)}, u32[]{:S(2)}) %copy-start.2) | copy-done | bytes 131096
  3.5 0.0 copy-start.3
  3.5 0.9 %copy-done.3 = bf16[192,256]{1,0:T(8,128)(2,1)S(1)} copy-done((bf16[192,256]{1,0:T(8,128)(2,1)S(1)}, bf16[192,256]{1,0:T(8,128)(2,1)}, u32[]{:S(2)}) %copy-start.3) | copy-done | bytes 98328
  4.3 0.0 copy-start.4
  4.3 0.8 %copy-done.4 = bf16[512,64]{0,1:T(8,128)(2,1)S(1)} copy-done((bf16[512,64]{0,1:T(8,128)(2,1)S(1)}, bf16[512,64]{0,1:T(8,128)(2,1)}, u32[]{:S(2)}) %copy-start.4) | copy-done | bytes 65560
  5.2 27.1 %shard_map.73 = bf16[256,256]{1,0:T(8,128)(2,1)S(1)} custom-call(s32[1,2]{1,0:T(1,128)S(1)} %copy-done.6, bf16[192,256]{1,0:T(8,128)(2,1)S(1)} %copy-done.3, bf16[256,256]{1,0:T(8,128)(2,1)S(1)} %copy-done.1, bf16[256,256]{1,0:T(8,128)(2,1)S(1)} %copy-done.2, s32[128,512]{1,0:T(8,128)S(1)} %bitcast.5, bf16[64,512]{1,0:T(8,128)(2,1)S(1)} %bitcast.6, ...), custom_call_target="tpu_custom_call" | custom-call | tf_op jit(solution)/shard_map/pallas_call | solution.py:303
  32.3 0.7 %copy.9 = bf16[256,256]{1,0:T(8,128)(2,1)} copy(bf16[256,256]{1,0:T(8,128)(2,1)S(1)} %shard_map.73) | data formatting | bytes 262144
Async XLA Ops:
  0.0 0.7 %copy-start.5 = (s32[512,2]{0,1:T(2,128)S(1)}, s32[512,2]{0,1:T(2,128)}, u32[]{:S(2)}) copy-start(s32[512,2]{0,1:T(2,128)} %param.13) | copy-start | bytes 12292
  0.0 0.7 %copy-start.6 = (s32[1,2]{1,0:T(1,128)S(1)}, s32[1,2]{1,0:T(1,128)}, u32[]{:S(2)}) copy-start(s32[1,2]{1,0:T(1,128)} %hit_ref.1) | copy-start | bytes 28
  0.7 1.0 %copy-start = (s32[512,2,64]{0,2,1:T(8,128)S(1)}, s32[512,2,64]{0,2,1:T(8,128)}, u32[]{:S(2)}) copy-start(s32[512,2,64]{0,2,1:T(8,128)} %param.11) | copy-start | bytes 786436
  1.6 0.9 %copy-start.1 = (bf16[256,256]{1,0:T(8,128)(2,1)S(1)}, bf16[256,256]{1,0:T(8,128)(2,1)}, u32[]{:S(2)}) copy-start(bf16[256,256]{1,0:T(8,128)(2,1)} %wv_hbm.1) | copy-start | bytes 393220
  2.5 0.9 %copy-start.2 = (bf16[256,256]{1,0:T(8,128)(2,1)S(1)}, bf16[256,256]{1,0:T(8,128)(2,1)}, u32[]{:S(2)}) copy-start(bf16[256,256]{1,0:T(8,128)(2,1)} %wo_hbm.1) | copy-start | bytes 393220
  3.5 0.9 %copy-start.3 = (bf16[192,256]{1,0:T(8,128)(2,1)S(1)}, bf16[192,256]{1,0:T(8,128)(2,1)}, u32[]{:S(2)}) copy-start(bf16[192,256]{1,0:T(8,128)(2,1)} %feat_hbm.1) | copy-start | bytes 294916
  4.3 0.8 %copy-start.4 = (bf16[512,64]{0,1:T(8,128)(2,1)S(1)}, bf16[512,64]{0,1:T(8,128)(2,1)}, u32[]{:S(2)}) copy-start(bf16[512,64]{0,1:T(8,128)(2,1)} %param.12) | copy-start | bytes 196612
